TPU v7x, 32 devices: a whole 2x2x4 slice. The times are simulated.
32 devices in a mesh: ta: 8 (over y, x, core), gz: 4 (over z).
Axes of the slice: x: 2, y: 2, z: 4, core: 2. Of those that a mesh axis runs over, the one named last changes fastest.
Arguments:
- source: bfloat16 [8, 4, 2, 4, 3, 12, 256], P('ta', 'gz'), may hold values from -6 to 6
- gauge_field: bfloat16 [8, 4, 4, 2, 3, 3, 256], P('ta', 'gz'), may hold values from -2.5 to 2.5
Outputs:
- twice_applied: bfloat16 [8, 4, 2, 4, 3, 12, 256], P('ta', 'gz')
All inputs are finite; a program needn't handle non-finite values.
Results may differ from a plain program's by a relative error of at most 0.0075.
Values may be sent and summed in bfloat16 or wider, within the bound.
A program may use at most 64 MiB of HBM per device.

v0:
```python
import functools

import jax
import jax.numpy as jnp
from jax import lax
from jax.experimental import pallas as pl
from jax.experimental.pallas import tpu as pltpu
from jax.sharding import PartitionSpec as P

NX = 16
HOPPING = 0.124
GAMMA_PERM = ((3, 2, 1, 0), (3, 2, 1, 0), (2, 3, 0, 1), (2, 3, 0, 1))
GAMMA_PHASE = (
    ((0, 1), (0, 1), (0, -1), (0, -1)),
    ((-1, 0), (1, 0), (1, 0), (-1, 0)),
    ((0, 1), (0, -1), (0, -1), (0, 1)),
    ((1, 0), (1, 0), (1, 0), (1, 0)),
)
LANES = 128
MESH = pl.DeviceIdType.MESH

HALOS = ((3, 1), (3, -1), (2, 1), (2, -1))


def signed_sum(base, term, sign):
    return base + term if sign > 0 else base - term


def rounded(first, second):
    return jnp.concatenate([first, second], 0).astype(jnp.bfloat16)


def project(psi, direction, hop_sign):
    out = []
    for s in range(2):
        partner = GAMMA_PERM[direction][s]
        pr, pi = GAMMA_PHASE[direction][s]
        row = []
        for c in range(3):
            if pi == 0:
                re = signed_sum(psi(0, s, c), psi(0, partner, c), -hop_sign * pr)
                im = signed_sum(psi(1, s, c), psi(1, partner, c), -hop_sign * pr)
            else:
                re = signed_sum(psi(0, s, c), psi(1, partner, c), hop_sign * pi)
                im = signed_sum(psi(1, s, c), psi(0, partner, c), -hop_sign * pi)
            row.append(rounded(re, im))
        out.append(row)
    return out


def widened(pair):
    wide = pair.astype(jnp.float32)
    return wide[:8], wide[8:]


def shift_sites(tile, direction, steps):
    lane = lax.broadcasted_iota(jnp.int32, (8, LANES), 1)
    if direction == 0:
        column = lane % NX
        if steps > 0:
            return jnp.where(
                column == NX - 1,
                pltpu.roll(tile, NX - 1, axis=1),
                pltpu.roll(tile, LANES - 1, axis=1),
            )
        return jnp.where(
            column == 0,
            pltpu.roll(tile, LANES - (NX - 1), axis=1),
            pltpu.roll(tile, 1, axis=1),
        )
    if steps > 0:
        near = pltpu.roll(tile, LANES - NX, axis=1)
        return jnp.where(lane >= LANES - NX, pltpu.roll(near, 4, axis=0), near)
    near = pltpu.roll(tile, NX, axis=1)
    return jnp.where(lane < NX, pltpu.roll(near, 4, axis=0), near)


def add_hop(acc, half, link, direction, hop_sign):
    for r in range(3):
        lr = [link(0, r, c) for c in range(3)]
        li = [link(1, r, c) for c in range(3)]
        k = []
        for s in range(2):
            re = im = None
            for c in range(3):
                hr, hi = half[s][c]
                tr = lr[c] * hr - li[c] * hi
                ti = lr[c] * hi + li[c] * hr
                re = tr if re is None else re + tr
                im = ti if im is None else im + ti
            k.append((re, im))
            acc[0][s][r] = acc[0][s][r] + re
            acc[1][s][r] = acc[1][s][r] + im
        for s in (2, 3):
            kr, ki = k[GAMMA_PERM[direction][s]]
            pr, pi = GAMMA_PHASE[direction][s]
            if pi == 0:
                acc[0][s][r] = signed_sum(acc[0][s][r], kr, -hop_sign * pr)
                acc[1][s][r] = signed_sum(acc[1][s][r], ki, -hop_sign * pr)
            else:
                acc[0][s][r] = signed_sum(acc[0][s][r], ki, hop_sign * pi)
                acc[1][s][r] = signed_sum(acc[1][s][r], kr, -hop_sign * pi)


def plane(ri, s, c):
    return (ri * 4 + s) * 3 + c


def link_slot(direction, hop_sign):
    return direction * 2 + (0 if hop_sign > 0 else 1)


def kernel(
    groups, source, gauge, out, psi, acc, links, sent, got, links_t, links_z,
    send_sem, recv_sem, link_send, link_recv,
):
    ta, gz = lax.axis_index("ta"), lax.axis_index("gz")
    nt, nz = lax.axis_size("ta"), lax.axis_size("gz")
    above_t = (lax.rem(ta + 1, nt), gz)
    below_t = (lax.rem(ta + nt - 1, nt), gz)
    above_z = (ta, lax.rem(gz + 1, nz))
    below_z = (ta, lax.rem(gz + nz - 1, nz))
    targets = (below_t, above_t, below_z, above_z)

    barrier = pltpu.get_barrier_semaphore()
    for target in targets:
        pl.semaphore_signal(barrier, inc=1, device_id=target, device_id_type=MESH)

    def halo_copy(step, halo, g):
        return pltpu.make_async_remote_copy(
            src_ref=sent.at[step, halo, g],
            dst_ref=got.at[step, halo, g],
            send_sem=send_sem.at[step, halo, g],
            recv_sem=recv_sem.at[step, halo, g],
            device_id=targets[halo],
            device_id_type=MESH,
        )

    def link_copy(which):
        return pltpu.make_async_remote_copy(
            src_ref=gauge.at[0, 0, 3 - which],
            dst_ref=(links_t, links_z)[which],
            send_sem=link_send.at[which],
            recv_sem=link_recv.at[which],
            device_id=(above_t, above_z)[which],
            device_id_type=MESH,
        )

    def put_halos(step, g, at):
        for halo, (direction, hop_sign) in enumerate(HALOS):
            half = project(at, direction, hop_sign)
            for s in range(2):
                for c in range(3):
                    sent[step, halo, g, pl.ds((s * 3 + c) * 16, 16)] = half[s][c]

    for p in range(24):
        rows = source[0, 0, p // 12, p // 3 % 4, p % 3].astype(jnp.float32)
        for g in range(groups):
            psi[0, g, p] = jnp.concatenate(
                [rows[4 * g : 4 * g + 4, :LANES], rows[4 * g : 4 * g + 4, LANES:]], 0
            )

    def load_psi(step, g):
        return lambda ri, s, c: psi[step, g, plane(ri, s, c)]

    def first_halos(g, carry):
        put_halos(0, g, load_psi(0, g))
        return carry

    lax.fori_loop(0, groups, first_halos, 0)
    pl.semaphore_wait(barrier, 4)
    for which in range(2):
        link_copy(which).start()

    def first_sends(g, carry):
        for halo in range(4):
            halo_copy(0, halo, g).start()
        return carry

    lax.fori_loop(0, groups, first_sends, 0)

    def spread(rows, c, scale):
        row = rows[c : c + 1] * scale
        return jnp.concatenate(
            [
                jnp.broadcast_to(row[:, :LANES], (4, LANES)),
                jnp.broadcast_to(row[:, LANES:], (4, LANES)),
            ],
            0,
        )

    def put_link(direction, hop_sign, ri, r, c, tile):
        if hop_sign > 0:
            links[link_slot(direction, 1), ri * 9 + r * 3 + c] = tile
        else:
            links[link_slot(direction, -1), ri * 9 + c * 3 + r] = tile if ri == 0 else -tile

    forward_scale = jnp.where(ta == nt - 1, HOPPING, -HOPPING).astype(jnp.float32)
    backward_scale = jnp.where(ta == 0, HOPPING, -HOPPING).astype(jnp.float32)
    for direction in range(4):
        scale = forward_scale if direction == 3 else jnp.float32(-HOPPING)
        for ri in range(2):
            for r in range(3):
                rows = gauge[0, 0, direction, ri, r].astype(jnp.float32)
                for c in range(3):
                    tile = spread(rows, c, scale)
                    put_link(direction, 1, ri, r, c, tile)
                    if direction < 2:
                        put_link(direction, -1, ri, r, c, shift_sites(tile, direction, -1))

    def load_link(direction, hop_sign):
        slot = link_slot(direction, hop_sign)
        return lambda ri, r, c: links[slot, ri * 9 + r * 3 + c]

    def load_spinor(at):
        return [[[at(ri, s, c) for c in range(3)] for s in range(4)] for ri in range(2)]

    def plane_hops(step):
        def body(g, carry):
            at = load_psi(step, g)
            total = load_spinor(at)
            for direction in (0, 1):
                for hop_sign in (1, -1):
                    pairs = project(at, direction, hop_sign)
                    half = [
                        [
                            tuple(shift_sites(v, direction, hop_sign) for v in widened(pairs[s][c]))
                            for c in range(3)
                        ]
                        for s in range(2)
                    ]
                    add_hop(total, half, load_link(direction, hop_sign), direction, hop_sign)
            for ri in range(2):
                for s in range(4):
                    for c in range(3):
                        acc[g, plane(ri, s, c)] = total[ri][s][c]
            return carry

        lax.fori_loop(0, groups, body, 0)

    def halo_hops(step):
        def body(g, carry):
            total = load_spinor(lambda ri, s, c: acc[g, plane(ri, s, c)])
            for halo, (direction, hop_sign) in enumerate(HALOS):
                halo_copy(step, halo, g).wait_recv()
                half = [
                    [widened(got[step, halo, g, pl.ds((s * 3 + c) * 16, 16)]) for c in range(3)]
                    for s in range(2)
                ]
                add_hop(total, half, load_link(direction, hop_sign), direction, hop_sign)
            final = {}
            for s in range(4):
                for c in range(3):
                    final[0, s, c], final[1, s, c] = widened(
                        rounded(total[0][s][c], total[1][s][c])
                    )
            for ri in range(2):
                for s in range(4):
                    for c in range(3):
                        psi[1 - step, g, plane(ri, s, c)] = final[ri, s, c]
            if step == 0:
                put_halos(1, g, lambda ri, s, c: final[ri, s, c])
                for halo in range(4):
                    halo_copy(1, halo, g).start()
            return carry

        lax.fori_loop(0, groups, body, 0)

    plane_hops(0)
    for which, scale in ((0, backward_scale), (1, jnp.float32(-HOPPING))):
        link_copy(which).wait_recv()
        for ri in range(2):
            for r in range(3):
                rows = (links_t, links_z)[which][ri, r].astype(jnp.float32)
                for c in range(3):
                    put_link(3 - which, -1, ri, r, c, spread(rows, c, scale))
    halo_hops(0)
    plane_hops(1)
    halo_hops(1)

    for p in range(24):
        rows = [psi[0, g, p] for g in range(groups)]
        low = jnp.concatenate([v[:4] for v in rows], 0)
        high = jnp.concatenate([v[4:] for v in rows], 0)
        out[0, 0, p // 12, p // 3 % 4, p % 3] = jnp.concatenate([low, high], 1).astype(jnp.bfloat16)

    def drain(g, carry):
        for step in range(2):
            for halo in range(4):
                halo_copy(step, halo, g).wait_send()
        return carry

    lax.fori_loop(0, groups, drain, 0)
    for which in range(2):
        link_copy(which).wait_send()


def body(source, gauge_field):
    groups = source.shape[5] // 4
    return pl.pallas_call(
        functools.partial(kernel, groups),
        out_shape=jax.ShapeDtypeStruct(source.shape, source.dtype),
        in_specs=[pl.BlockSpec(memory_space=pltpu.VMEM)] * 2,
        out_specs=pl.BlockSpec(memory_space=pltpu.VMEM),
        scratch_shapes=[
            pltpu.VMEM((2, groups, 24, 8, LANES), jnp.float32),
            pltpu.VMEM((groups, 24, 8, LANES), jnp.float32),
            pltpu.VMEM((8, 18, 8, LANES), jnp.float32),
            pltpu.VMEM((2, 4, groups, 96, LANES), jnp.bfloat16),
            pltpu.VMEM((2, 4, groups, 96, LANES), jnp.bfloat16),
            pltpu.VMEM(gauge_field.shape[3:], jnp.bfloat16),
            pltpu.VMEM(gauge_field.shape[3:], jnp.bfloat16),
            pltpu.SemaphoreType.DMA((2, 4, groups)),
            pltpu.SemaphoreType.DMA((2, 4, groups)),
            pltpu.SemaphoreType.DMA((2,)),
            pltpu.SemaphoreType.DMA((2,)),
        ],
        compiler_params=pltpu.CompilerParams(collective_id=0, has_side_effects=True),
        name="dirac_twice",
    )(source, gauge_field)


def solution(mesh):
    spec = P("ta", "gz", None, None, None, None, None)
    return jax.shard_map(body, mesh=mesh, in_specs=(spec, spec), out_specs=spec, check_vma=False)
```

profile of v0, /device:TPU:0, one launch (start us, length us, event | category | flops | bytes accessed | tf_op | source)
XLA Modules:
  0.0 21.7 jit_solution(3738827768281483258)
XLA Ops:
  0.0 1.4 %copy.4.gauge = bf16[1,1,4,2,3,3,256]{6,5,4,3,2,1,0:T(4,128)(2,1)} copy(bf16[1,1,4,2,3,3,256]{6,3,5,4,2,1,0:T(2,128)(2,1)} %param.3) | data formatting | bytes 73728 | tf_op args[1]
  1.4 1.6 %copy.3.source = bf16[1,1,2,4,3,12,256]{6,5,4,3,2,1,0:T(8,128)(2,1)} copy(bf16[1,1,2,4,3,12,256]{6,3,5,4,2,1,0:T(4,128)(2,1)} %param.2) | data formatting | bytes 294912 | tf_op args[0]
  3.0 17.0 %dirac_twice.1 = bf16[1,1,2,4,3,12,256]{6,5,4,3,2,1,0:T(8,128)(2,1)} custom-call(bf16[1,1,2,4,3,12,256]{6,5,4,3,2,1,0:T(8,128)(2,1)} %copy.3.source, bf16[1,1,4,2,3,3,256]{6,5,4,3,2,1,0:T(4,128)(2,1)} %copy.4.gauge), custom_call_target="tpu_custom_call" | custom-call | tf_op jit(solution)/shard_map/dirac_twice/pallas_call | solution.py:300
  20.0 1.7 %copy.5 = bf16[1,1,2,4,3,12,256]{6,3,5,4,2,1,0:T(4,128)(2,1)} copy(bf16[1,1,2,4,3,12,256]{6,5,4,3,2,1,0:T(8,128)(2,1)} %dirac_twice.1) | data formatting | bytes 294912 | tf_op jit(solution)/shard_map/dirac_twice/pallas_call | solution.py:300
where the time goes:
time: 21.9 us; the launch traced here: 21.7 us
  Pallas kernels  17 us (78%)
  local copies, waits for them, and re-layouts  4.67 us (21%)
    pallas_call x1, Pallas kernels, body(): pl.pallas_call(functools.partial(kernel, groups), out_shape=jax.ShapeDtyp...  17 us
    unnamed x2, local copies, waits for them, and re-layouts  3.01 us
    pallas_call x1, local copies, waits for them, and re-layouts, body(): pl.pallas_call(functools.partial(kernel, groups), out_shape=jax.ShapeDtyp...  1.66 us

commit v1 on v0

--- a/solution.py
+++ b/solution.py
@@ -68,11 +68,10 @@
             pltpu.roll(tile, LANES - (NX - 1), axis=1),
             pltpu.roll(tile, 1, axis=1),
         )
-    if steps > 0:
-        near = pltpu.roll(tile, LANES - NX, axis=1)
-        return jnp.where(lane >= LANES - NX, pltpu.roll(near, 4, axis=0), near)
-    near = pltpu.roll(tile, NX, axis=1)
-    return jnp.where(lane < NX, pltpu.roll(near, 4, axis=0), near)
+    near = pltpu.roll(tile, LANES - NX if steps > 0 else NX, axis=1)
+    first_half = lax.broadcasted_iota(jnp.int32, (8, LANES), 0) % 2 == 0
+    other = jnp.where(first_half, pltpu.roll(near, 7, axis=0), pltpu.roll(near, 1, axis=0))
+    return jnp.where(lane >= LANES - NX if steps > 0 else lane < NX, other, near)
 
 
 def add_hop(acc, half, link, direction, hop_sign):
@@ -111,8 +110,8 @@
 
 
 def kernel(
-    groups, source, gauge, out, psi, acc, links, sent, got, links_t, links_z,
-    send_sem, recv_sem, link_send, link_recv,
+    groups, source_hbm, gauge_hbm, out, source, gauge, wide, psi, acc, links, sent, got,
+    links_below, load_sem, send_sem, recv_sem, link_send, link_recv,
 ):
     ta, gz = lax.axis_index("ta"), lax.axis_index("gz")
     nt, nz = lax.axis_size("ta"), lax.axis_size("gz")
@@ -122,6 +121,10 @@
     below_z = (ta, lax.rem(gz + nz - 1, nz))
     targets = (below_t, above_t, below_z, above_z)
 
+    source_load = pltpu.make_async_copy(source_hbm, source, load_sem.at[0])
+    gauge_load = pltpu.make_async_copy(gauge_hbm, gauge, load_sem.at[1])
+    source_load.start()
+    gauge_load.start()
     barrier = pltpu.get_barrier_semaphore()
     for target in targets:
         pl.semaphore_signal(barrier, inc=1, device_id=target, device_id_type=MESH)
@@ -138,8 +141,8 @@
 
     def link_copy(which):
         return pltpu.make_async_remote_copy(
-            src_ref=gauge.at[0, 0, 3 - which],
-            dst_ref=(links_t, links_z)[which],
+            src_ref=gauge_hbm.at[pl.ds(9 * (3 - which), 9)],
+            dst_ref=links_below.at[which],
             send_sem=link_send.at[which],
             recv_sem=link_recv.at[which],
             device_id=(above_t, above_z)[which],
@@ -153,12 +156,17 @@
                 for c in range(3):
                     sent[step, halo, g, pl.ds((s * 3 + c) * 16, 16)] = half[s][c]
 
-    for p in range(24):
-        rows = source[0, 0, p // 12, p // 3 % 4, p % 3].astype(jnp.float32)
-        for g in range(groups):
-            psi[0, g, p] = jnp.concatenate(
-                [rows[4 * g : 4 * g + 4, :LANES], rows[4 * g : 4 * g + 4, LANES:]], 0
-            )
+    def rows_of(ri, s, c, g):
+        return pl.ds(((ri * 3 + c) * groups + g) * 32 + s, 8, stride=4)
+
+    source_load.wait()
+    for p in range(source.shape[0]):
+        wide[8 * p : 8 * p + 8] = source[p].astype(jnp.float32)
+    for g in range(groups):
+        for ri in range(2):
+            for s in range(4):
+                for c in range(3):
+                    psi[0, g, plane(ri, s, c)] = wide[rows_of(ri, s, c, g)]
 
     def load_psi(step, g):
         return lambda ri, s, c: psi[step, g, plane(ri, s, c)]
@@ -179,14 +187,13 @@
 
     lax.fori_loop(0, groups, first_sends, 0)
 
-    def spread(rows, c, scale):
-        row = rows[c : c + 1] * scale
-        return jnp.concatenate(
-            [
-                jnp.broadcast_to(row[:, :LANES], (4, LANES)),
-                jnp.broadcast_to(row[:, LANES:], (4, LANES)),
-            ],
-            0,
+    first_half = lax.broadcasted_iota(jnp.int32, (8, LANES), 0) % 2 == 0
+
+    def spread(rows, ri, scale):
+        return scale * jnp.where(
+            first_half,
+            jnp.broadcast_to(rows[ri : ri + 1], (8, LANES)),
+            jnp.broadcast_to(rows[2 + ri : 3 + ri], (8, LANES)),
         )
 
     def put_link(direction, hop_sign, ri, r, c, tile):
@@ -197,13 +204,14 @@
 
     forward_scale = jnp.where(ta == nt - 1, HOPPING, -HOPPING).astype(jnp.float32)
     backward_scale = jnp.where(ta == 0, HOPPING, -HOPPING).astype(jnp.float32)
+    gauge_load.wait()
     for direction in range(4):
         scale = forward_scale if direction == 3 else jnp.float32(-HOPPING)
-        for ri in range(2):
-            for r in range(3):
-                rows = gauge[0, 0, direction, ri, r].astype(jnp.float32)
-                for c in range(3):
-                    tile = spread(rows, c, scale)
+        for r in range(3):
+            for c in range(3):
+                rows = gauge[direction * 9 + r * 3 + c].astype(jnp.float32)
+                for ri in range(2):
+                    tile = spread(rows, ri, scale)
                     put_link(direction, 1, ri, r, c, tile)
                     if direction < 2:
                         put_link(direction, -1, ri, r, c, shift_sites(tile, direction, -1))
@@ -254,14 +262,20 @@
                     final[0, s, c], final[1, s, c] = widened(
                         rounded(total[0][s][c], total[1][s][c])
                     )
-            for ri in range(2):
-                for s in range(4):
-                    for c in range(3):
-                        psi[1 - step, g, plane(ri, s, c)] = final[ri, s, c]
+            for (ri, s, c), tile in final.items():
+                if step == 0:
+                    psi[1, g, plane(ri, s, c)] = tile
+                else:
+                    wide[rows_of(ri, s, c, g)] = tile
             if step == 0:
                 put_halos(1, g, lambda ri, s, c: final[ri, s, c])
                 for halo in range(4):
                     halo_copy(1, halo, g).start()
+            else:
+                for block in range(6):
+                    for p in range(4):
+                        at = (block * groups + g) * 4 + p
+                        out[at] = wide[pl.ds(8 * at, 8)].astype(jnp.bfloat16)
             return carry
 
         lax.fori_loop(0, groups, body, 0)
@@ -269,20 +283,14 @@
     plane_hops(0)
     for which, scale in ((0, backward_scale), (1, jnp.float32(-HOPPING))):
         link_copy(which).wait_recv()
-        for ri in range(2):
-            for r in range(3):
-                rows = (links_t, links_z)[which][ri, r].astype(jnp.float32)
-                for c in range(3):
-                    put_link(3 - which, -1, ri, r, c, spread(rows, c, scale))
+        for r in range(3):
+            for c in range(3):
+                rows = links_below[which, r * 3 + c].astype(jnp.float32)
+                for ri in range(2):
+                    put_link(3 - which, -1, ri, r, c, spread(rows, ri, scale))
     halo_hops(0)
     plane_hops(1)
     halo_hops(1)
-
-    for p in range(24):
-        rows = [psi[0, g, p] for g in range(groups)]
-        low = jnp.concatenate([v[:4] for v in rows], 0)
-        high = jnp.concatenate([v[4:] for v in rows], 0)
-        out[0, 0, p // 12, p // 3 % 4, p % 3] = jnp.concatenate([low, high], 1).astype(jnp.bfloat16)
 
     def drain(g, carry):
         for step in range(2):
@@ -296,20 +304,28 @@
 
 
 def body(source, gauge_field):
-    groups = source.shape[5] // 4
-    return pl.pallas_call(
+    rhs = source.shape[5]
+    groups = rhs // 4
+    source_rows = source.reshape(2, 4, 3, rhs, 2, LANES).transpose(0, 2, 3, 4, 1, 5)
+    source_rows = source_rows.reshape(6 * rhs, 8, LANES)
+    gauge_rows = gauge_field.reshape(4, 2, 3, 3, 2, LANES).transpose(0, 2, 3, 4, 1, 5)
+    gauge_rows = gauge_rows.reshape(36, 4, LANES)
+    rows = pl.pallas_call(
         functools.partial(kernel, groups),
-        out_shape=jax.ShapeDtypeStruct(source.shape, source.dtype),
-        in_specs=[pl.BlockSpec(memory_space=pltpu.VMEM)] * 2,
+        out_shape=jax.ShapeDtypeStruct(source_rows.shape, source.dtype),
+        in_specs=[pl.BlockSpec(memory_space=pltpu.HBM)] * 2,
         out_specs=pl.BlockSpec(memory_space=pltpu.VMEM),
         scratch_shapes=[
+            pltpu.VMEM(source_rows.shape, jnp.bfloat16),
+            pltpu.VMEM(gauge_rows.shape, jnp.bfloat16),
+            pltpu.VMEM((48 * rhs, LANES), jnp.float32),
             pltpu.VMEM((2, groups, 24, 8, LANES), jnp.float32),
             pltpu.VMEM((groups, 24, 8, LANES), jnp.float32),
             pltpu.VMEM((8, 18, 8, LANES), jnp.float32),
             pltpu.VMEM((2, 4, groups, 96, LANES), jnp.bfloat16),
             pltpu.VMEM((2, 4, groups, 96, LANES), jnp.bfloat16),
-            pltpu.VMEM(gauge_field.shape[3:], jnp.bfloat16),
-            pltpu.VMEM(gauge_field.shape[3:], jnp.bfloat16),
+            pltpu.VMEM((2, 9, 4, LANES), jnp.bfloat16),
+            pltpu.SemaphoreType.DMA((2,)),
             pltpu.SemaphoreType.DMA((2, 4, groups)),
             pltpu.SemaphoreType.DMA((2, 4, groups)),
             pltpu.SemaphoreType.DMA((2,)),
@@ -317,7 +333,9 @@
         ],
         compiler_params=pltpu.CompilerParams(collective_id=0, has_side_effects=True),
         name="dirac_twice",
-    )(source, gauge_field)
+    )(source_rows, gauge_rows)
+    out = rows.reshape(2, 3, rhs, 2, 4, LANES).transpose(0, 4, 1, 2, 3, 5)
+    return out.reshape(source.shape)
 
 
 def solution(mesh):

time: 21.9 us -> 17.8 us (0.81)
  local copies, waits for them, and re-layouts: 4.67 us -> 1.62 us
  Pallas kernels: 17 us -> 16.1 us
    pallas_call x1 -> x0, local copies, waits for them, and re-layouts: 1.66 us -> none  [body(): pl.pallas_call(functools.partial(kernel, groups), out_shape=jax.ShapeDtyp...]
    unnamed x2 -> x1, local copies, waits for them, and re-layouts: 3.01 us -> 1.62 us
    pallas_call x1, Pallas kernels: 17 us -> 16.1 us  [body(): pl.pallas_call(functools.partial(kernel, groups), out_shape=jax.ShapeDtyp...]
where the time goes in v1:
time: 17.8 us; the launch traced here: 17.7 us
  Pallas kernels  16.1 us (90%)
  local copies, waits for them, and re-layouts  1.62 us (9%)
    pallas_call x1, Pallas kernels, body(): pl.pallas_call(functools.partial(kernel, groups), out_shape=jax.ShapeDtyp...  16.1 us
    unnamed x1, local copies, waits for them, and re-layouts  1.62 us

profile of v1, /device:TPU:0, one launch (start us, length us, event | category | flops | bytes accessed | tf_op | source)
XLA Modules:
  0.0 17.7 jit_solution(12159731319303441332)
XLA Ops:
  0.0 16.1 %dirac_twice.1 = bf16[72,8,128]{2,1,0:T(8,128)(2,1)} custom-call(bf16[72,8,128]{2,1,0:T(8,128)(2,1)} %bitcast.16, bf16[36,4,128]{2,1,0:T(4,128)(2,1)} %bitcast.17), custom_call_target="tpu_custom_call" | custom-call | tf_op jit(solution)/shard_map/dirac_twice/pallas_call | solution.py:313
  16.1 1.6 %copy.7 = bf16[1,1,2,4,3,12,256]{6,3,5,4,2,1,0:T(4,128)(2,1)} copy(bf16[1,1,2,4,3,12,256]{6,3,5,4,2,1,0:T(4,128)(2,1)} %bitcast.15) | data formatting | bytes 294912

commit v2 on v1

--- a/solution.py
+++ b/solution.py
@@ -23,6 +23,8 @@
 
 
 def signed_sum(base, term, sign):
+    if not isinstance(sign, int):
+        return base + term * sign
     return base + term if sign > 0 else base - term
 
 
@@ -129,13 +131,21 @@
     for target in targets:
         pl.semaphore_signal(barrier, inc=1, device_id=target, device_id_type=MESH)
 
+    upper = (2 * gz) // nz
+    early, late = 2 + upper, 3 - upper
+    early_sign = (1 - 2 * upper).astype(jnp.float32)
+
     def halo_copy(step, halo, g):
+        if isinstance(halo, int):
+            target = targets[halo]
+        else:
+            target = (ta, lax.rem(gz + (3 - halo) * (nz - 1) + (halo - 2), nz))
         return pltpu.make_async_remote_copy(
             src_ref=sent.at[step, halo, g],
             dst_ref=got.at[step, halo, g],
             send_sem=send_sem.at[step, halo, g],
             recv_sem=recv_sem.at[step, halo, g],
-            device_id=targets[halo],
+            device_id=target,
             device_id_type=MESH,
         )
 
@@ -181,10 +191,12 @@
         link_copy(which).start()
 
     def first_sends(g, carry):
-        for halo in range(4):
+        for halo in (0, 1, late):
             halo_copy(0, halo, g).start()
         return carry
 
+    for g in range(groups):
+        halo_copy(0, early, g).start()
     lax.fori_loop(0, groups, first_sends, 0)
 
     first_half = lax.broadcasted_iota(jnp.int32, (8, LANES), 0) % 2 == 0
@@ -246,16 +258,41 @@
 
         lax.fori_loop(0, groups, body, 0)
 
+    def add_halo(total, step, halo, g, link, direction, hop_sign):
+        halo_copy(step, halo, g).wait_recv()
+        half = [
+            [widened(got[step, halo, g, pl.ds((s * 3 + c) * 16, 16)]) for c in range(3)]
+            for s in range(2)
+        ]
+        add_hop(total, half, link, direction, hop_sign)
+
+    def slot_link(slot):
+        return lambda ri, r, c: links[slot, ri * 9 + r * 3 + c]
+
+    def early_hops(g, carry):
+        total = load_spinor(lambda ri, s, c: acc[g, plane(ri, s, c)])
+        for halo, (direction, hop_sign) in enumerate(HALOS[:2]):
+            add_halo(total, 0, halo, g, load_link(direction, hop_sign), direction, hop_sign)
+        add_halo(total, 0, early, g, slot_link(4 + upper), 2, early_sign)
+        half = project(lambda ri, s, c: total[ri][s][c], 2, early_sign)
+        for s in range(2):
+            for c in range(3):
+                sent[1, early, g, pl.ds((s * 3 + c) * 16, 16)] = half[s][c]
+        for ri in range(2):
+            for s in range(4):
+                for c in range(3):
+                    acc[g, plane(ri, s, c)] = total[ri][s][c]
+        halo_copy(1, early, g).start()
+        return carry
+
     def halo_hops(step):
         def body(g, carry):
             total = load_spinor(lambda ri, s, c: acc[g, plane(ri, s, c)])
-            for halo, (direction, hop_sign) in enumerate(HALOS):
-                halo_copy(step, halo, g).wait_recv()
-                half = [
-                    [widened(got[step, halo, g, pl.ds((s * 3 + c) * 16, 16)]) for c in range(3)]
-                    for s in range(2)
-                ]
-                add_hop(total, half, load_link(direction, hop_sign), direction, hop_sign)
+            if step == 0:
+                add_halo(total, 0, late, g, slot_link(5 - upper), 2, -early_sign)
+            else:
+                for halo, (direction, hop_sign) in enumerate(HALOS):
+                    add_halo(total, 1, halo, g, load_link(direction, hop_sign), direction, hop_sign)
             final = {}
             for s in range(4):
                 for c in range(3):
@@ -268,8 +305,15 @@
                 else:
                     wide[rows_of(ri, s, c, g)] = tile
             if step == 0:
-                put_halos(1, g, lambda ri, s, c: final[ri, s, c])
-                for halo in range(4):
+                at = lambda ri, s, c: final[ri, s, c]
+                halves = (
+                    (0, project(at, 3, 1)), (1, project(at, 3, -1)), (late, project(at, 2, -early_sign))
+                )
+                for halo, half in halves:
+                    for s in range(2):
+                        for c in range(3):
+                            sent[1, halo, g, pl.ds((s * 3 + c) * 16, 16)] = half[s][c]
+                for halo, _ in halves:
                     halo_copy(1, halo, g).start()
             else:
                 for block in range(6):
@@ -288,6 +332,7 @@
                 rows = links_below[which, r * 3 + c].astype(jnp.float32)
                 for ri in range(2):
                     put_link(3 - which, -1, ri, r, c, spread(rows, ri, scale))
+    lax.fori_loop(0, groups, early_hops, 0)
     halo_hops(0)
     plane_hops(1)
     halo_hops(1)
@@ -312,7 +357,7 @@
     gauge_rows = gauge_rows.reshape(36, 4, LANES)
     rows = pl.pallas_call(
         functools.partial(kernel, groups),
-        out_shape=jax.ShapeDtypeStruct(source_rows.shape, source.dtype),
+        out_shape=pltpu.VMEM(source_rows.shape, source.dtype),
         in_specs=[pl.BlockSpec(memory_space=pltpu.HBM)] * 2,
         out_specs=pl.BlockSpec(memory_space=pltpu.VMEM),
         scratch_shapes=[

time: 17.8 us -> 14.6 us (0.82)
  Pallas kernels: 16.1 us -> 13.8 us
  local copies, waits for them, and re-layouts: 1.62 us -> 0.66 us
    pallas_call x1, Pallas kernels: 16.1 us -> 13.8 us  [body(): pl.pallas_call(functools.partial(kernel, groups), out_shape=pltpu.VMEM(so...]
    unnamed x1, local copies, waits for them, and re-layouts: 1.62 us -> 0.66 us
where the time goes in v2:
time: 14.6 us; the launch traced here: 14.4 us
  Pallas kernels  13.8 us (95%)
  local copies, waits for them, and re-layouts  0.66 us (5%)
    pallas_call x1, Pallas kernels, body(): pl.pallas_call(functools.partial(kernel, groups), out_shape=pltpu.VMEM(so...  13.8 us
    unnamed x1, local copies, waits for them, and re-layouts  0.66 us

profile of v2, /device:TPU:0, one launch (start us, length us, event | category | flops | bytes accessed | tf_op | source)
XLA Modules:
  0.0 14.4 jit_solution(2809965849707864491)
XLA Ops:
  0.0 13.8 %dirac_twice.1 = bf16[72,8,128]{2,1,0:T(8,128)(2,1)S(1)} custom-call(bf16[72,8,128]{2,1,0:T(8,128)(2,1)} %bitcast.16, bf16[36,4,128]{2,1,0:T(4,128)(2,1)} %bitcast.17), custom_call_target="tpu_custom_call" | custom-call | tf_op jit(solution)/shard_map/dirac_twice/pallas_call | solution.py:358
  13.8 0.7 %copy.7 = bf16[1,1,2,4,3,12,256]{6,3,5,4,2,1,0:T(4,128)(2,1)} copy(bf16[1,1,2,4,3,12,256]{6,3,5,4,2,1,0:T(4,128)(2,1)S(1)} %bitcast.15) | data formatting | bytes 294912

commit v3 on v2

--- a/solution.py
+++ b/solution.py
@@ -151,7 +151,7 @@
 
     def link_copy(which):
         return pltpu.make_async_remote_copy(
-            src_ref=gauge_hbm.at[pl.ds(9 * (3 - which), 9)],
+            src_ref=gauge.at[pl.ds(9 * (3 - which), 9)],
             dst_ref=links_below.at[which],
             send_sem=link_send.at[which],
             recv_sem=link_recv.at[which],
@@ -186,16 +186,18 @@
         return carry
 
     lax.fori_loop(0, groups, first_halos, 0)
+    gauge_load.wait()
     pl.semaphore_wait(barrier, 4)
-    for which in range(2):
-        link_copy(which).start()
 
     def first_sends(g, carry):
         for halo in (0, 1, late):
             halo_copy(0, halo, g).start()
         return carry
 
-    for g in range(groups):
+    halo_copy(0, early, 0).start()
+    for which in range(2):
+        link_copy(which).start()
+    for g in range(1, groups):
         halo_copy(0, early, g).start()
     lax.fori_loop(0, groups, first_sends, 0)
 
@@ -216,7 +218,6 @@
 
     forward_scale = jnp.where(ta == nt - 1, HOPPING, -HOPPING).astype(jnp.float32)
     backward_scale = jnp.where(ta == 0, HOPPING, -HOPPING).astype(jnp.float32)
-    gauge_load.wait()
     for direction in range(4):
         scale = forward_scale if direction == 3 else jnp.float32(-HOPPING)
         for r in range(3):
@@ -325,14 +326,17 @@
         lax.fori_loop(0, groups, body, 0)
 
     plane_hops(0)
-    for which, scale in ((0, backward_scale), (1, jnp.float32(-HOPPING))):
+    def take_links(which, scale):
         link_copy(which).wait_recv()
         for r in range(3):
             for c in range(3):
                 rows = links_below[which, r * 3 + c].astype(jnp.float32)
                 for ri in range(2):
                     put_link(3 - which, -1, ri, r, c, spread(rows, ri, scale))
+    take_links(0, backward_scale)
+    pl.when(upper == 1)(lambda: take_links(1, jnp.float32(-HOPPING)))
     lax.fori_loop(0, groups, early_hops, 0)
+    pl.when(upper == 0)(lambda: take_links(1, jnp.float32(-HOPPING)))
     halo_hops(0)
     plane_hops(1)
     halo_hops(1)

time: 14.6 us -> 14.6 us (level)
  no operation moved by 1% of the time
where the time goes in v3:
time: 14.6 us; the launch traced here: 14.5 us
  Pallas kernels  13.8 us (95%)
  local copies, waits for them, and re-layouts  0.66 us (5%)
    pallas_call x1, Pallas kernels, body(): pl.pallas_call(functools.partial(kernel, groups), out_shape=pltpu.VMEM(so...  13.8 us
    unnamed x1, local copies, waits for them, and re-layouts  0.66 us

profile of v3, /device:TPU:0, one launch (start us, length us, event | category | flops | bytes accessed | tf_op | source)
XLA Modules:
  0.0 14.5 jit_solution(4273446326985222510)
XLA Ops:
  0.0 13.8 %dirac_twice.1 = bf16[72,8,128]{2,1,0:T(8,128)(2,1)S(1)} custom-call(bf16[72,8,128]{2,1,0:T(8,128)(2,1)} %bitcast.16, bf16[36,4,128]{2,1,0:T(4,128)(2,1)} %bitcast.17), custom_call_target="tpu_custom_call" | custom-call | tf_op jit(solution)/shard_map/dirac_twice/pallas_call | solution.py:362
  13.8 0.7 %copy.7 = bf16[1,1,2,4,3,12,256]{6,3,5,4,2,1,0:T(4,128)(2,1)} copy(bf16[1,1,2,4,3,12,256]{6,3,5,4,2,1,0:T(4,128)(2,1)S(1)} %bitcast.15) | data formatting | bytes 294912
